TPU v7x, 32 devices: a whole 2x2x4 slice. The times are simulated.
32 devices in a mesh: mod: 4 (over x, core), shard: 8 (over z, y).
Axes of the slice: x: 2, y: 2, z: 4, core: 2. Of those that a mesh axis runs over, the one named last changes fastest.
Arguments:
- tokens_b: bfloat16 [512, 4096], P(('mod', 'shard')), may hold values from -6 to 6
- labels_b: int32 [512, 1], P(('mod', 'shard')), may hold values from 0 to 3; in each aligned block of 16 rows (0 to 15, 16 to 31, ...) at most 6 rows name the same one
- tokens_a: bfloat16 [512, 4096], P(('mod', 'shard')), may hold values from -6 to 6
- labels_a: int32 [512, 1], P(('mod', 'shard')), may hold values from 0 to 3; in each aligned block of 16 rows (0 to 15, 16 to 31, ...) at most 6 rows name the same one
- grad_out_a: bfloat16 [512, 4096], P(('mod', 'shard')), may hold values from -6 to 6
- gate_saved: bfloat16 [4, 192, 11008], P('mod', None, 'shard'), may hold values from -6 to 6
- up_saved: bfloat16 [4, 192, 11008], P('mod', None, 'shard'), may hold values from -6 to 6
- gate_weight: bfloat16 [4, 4096, 11008], P('mod', None, 'shard'), may hold values from -0.09375 to 0.09375
- up_weight: bfloat16 [4, 4096, 11008], P('mod', None, 'shard'), may hold values from -0.09375 to 0.09375
- down_weight: bfloat16 [4, 11008, 4096], P('mod', 'shard'), may hold values from -0.0546875 to 0.0546875
Outputs:
- output_b: bfloat16 [512, 4096], P(('mod', 'shard'))
- grad_tokens_a: bfloat16 [512, 4096], P(('mod', 'shard'))
- grad_gate: bfloat16 [4, 4096, 11008], P('mod', None, 'shard')
- grad_up: bfloat16 [4, 4096, 11008], P('mod', None, 'shard')
- grad_down: bfloat16 [4, 11008, 4096], P('mod', 'shard')
Inputs may be any that keep to these rules, and one draw needn't show every extreme that they name: `labels_b`: among the 16 tokens of one home device no label occurs more than 6 times; in every draw some home device has exactly 6 tokens of one label. `labels_a`: among the 16 tokens of one home device no label occurs more than 6 times; in every draw some home device has exactly 6 tokens of one label.
All inputs are finite; a program needn't handle non-finite values.
Results may differ from a plain program's by a relative error of at most 0.0049.
Values may be sent and summed in bfloat16 or wider, within the bound.
A program may use at most 128 MiB of HBM per device.

v0:
```python
import jax
import jax.numpy as jnp
from jax import lax
from jax.sharding import PartitionSpec as P

CAP = 6


def place_table(labels, modes):
    lab = labels[:, 0]
    onehot = (lab[:, None] == jnp.arange(modes, dtype=jnp.int32)[None, :]).astype(jnp.int32)
    rank = jnp.cumsum(onehot, axis=0) - onehot
    slot = jnp.sum(rank * onehot, axis=1)
    within = (slot[:, None] == jnp.arange(CAP, dtype=jnp.int32)[None, :]).astype(jnp.int32)
    table = onehot[:, :, None] * within[:, None, :]
    return table.reshape(lab.shape[0], modes * CAP).astype(jnp.bfloat16)


def dispatch(place, values, modes):
    sent = lax.dot_general(
        place, values, (((0,), (0,)), ((), ())), preferred_element_type=jnp.float32
    )
    return sent.astype(jnp.bfloat16).reshape(modes, CAP, values.shape[1])


def collect(place, arrived):
    flat = arrived.reshape(place.shape[1], arrived.shape[2])
    return jnp.dot(place, flat, preferred_element_type=jnp.float32).astype(jnp.bfloat16)


def contract_last(left, right):
    return lax.dot_general(
        left, right, (((1,), (1,)), ((), ())), preferred_element_type=jnp.float32
    )


def forward_pass(tokens_b, labels_b, gate_w, up_w, down_w):
    modes = lax.axis_size("mod")
    width = tokens_b.shape[1]
    place = place_table(labels_b, modes)
    sent = dispatch(place, tokens_b, modes)
    arrived = lax.all_to_all(sent, "mod", split_axis=0, concat_axis=0, tiled=True)
    local_rows = arrived.reshape(modes * CAP, width)
    piece = lax.all_gather(local_rows, "shard", axis=0, tiled=True)
    gate = jnp.dot(piece, gate_w, preferred_element_type=jnp.float32)
    up = jnp.dot(piece, up_w, preferred_element_type=jnp.float32)
    terms = jnp.dot(
        (jax.nn.silu(gate) * up).astype(jnp.bfloat16), down_w, preferred_element_type=jnp.float32
    )
    summed = lax.psum_scatter(terms, "shard", scatter_dimension=0, tiled=True)
    back = summed.astype(jnp.bfloat16).reshape(modes, CAP, width)
    returned = lax.all_to_all(back, "mod", split_axis=0, concat_axis=0, tiled=True)
    return collect(place, returned)


def backward_pass(tokens_a, labels_a, grad_out_a, gate_s, up_s, gate_w, up_w, down_w):
    modes = lax.axis_size("mod")
    width = tokens_a.shape[1]
    place = place_table(labels_a, modes)
    sent_x = dispatch(place, tokens_a, modes)
    sent_g = dispatch(place, grad_out_a, modes)
    arrived_x, arrived_g = (
        lax.all_to_all(sent_x, "mod", split_axis=0, concat_axis=0, tiled=True),
        lax.all_to_all(sent_g, "mod", split_axis=0, concat_axis=0, tiled=True),
    )
    all_x, all_g = (
        lax.all_gather(arrived_x.reshape(modes * CAP, width), "shard", axis=0, tiled=True),
        lax.all_gather(arrived_g.reshape(modes * CAP, width), "shard", axis=0, tiled=True),
    )
    gate = gate_s.astype(jnp.float32)
    up = up_s.astype(jnp.float32)
    sig = jax.nn.sigmoid(gate)
    act = gate * sig
    dh = contract_last(all_g, down_w)
    dgate = (dh * up * sig * (1.0 + gate * (1.0 - sig))).astype(jnp.bfloat16)
    dup = (dh * act).astype(jnp.bfloat16)
    hidden = (act * up).astype(jnp.bfloat16)
    outer = (((0,), (0,)), ((), ()))
    grad_down = lax.dot_general(hidden, all_g, outer, preferred_element_type=jnp.float32).astype(
        jnp.bfloat16
    )
    grad_gate = lax.dot_general(all_x, dgate, outer, preferred_element_type=jnp.float32).astype(
        jnp.bfloat16
    )
    grad_up = lax.dot_general(all_x, dup, outer, preferred_element_type=jnp.float32).astype(
        jnp.bfloat16
    )
    terms = contract_last(dgate, gate_w) + contract_last(dup, up_w)
    summed = lax.psum_scatter(terms, "shard", scatter_dimension=0, tiled=True)
    back = summed.astype(jnp.bfloat16).reshape(modes, CAP, width)
    returned = lax.all_to_all(back, "mod", split_axis=0, concat_axis=0, tiled=True)
    return (collect(place, returned), grad_gate[None], grad_up[None], grad_down[None])


def body(
    tokens_b,
    labels_b,
    tokens_a,
    labels_a,
    grad_out_a,
    gate_saved,
    up_saved,
    gate_weight,
    up_weight,
    down_weight,
):
    gate_w = gate_weight[0]
    up_w = up_weight[0]
    down_w = down_weight[0]
    output_b = forward_pass(tokens_b, labels_b, gate_w, up_w, down_w)
    grads = backward_pass(
        tokens_a, labels_a, grad_out_a, gate_saved[0], up_saved[0], gate_w, up_w, down_w
    )
    return (output_b, grads[0], grads[1], grads[2], grads[3])


def solution(mesh):
    return jax.shard_map(
        body,
        mesh=mesh,
        in_specs=(
            P(("mod", "shard"), None),
            P(("mod", "shard"), None),
            P(("mod", "shard"), None),
            P(("mod", "shard"), None),
            P(("mod", "shard"), None),
            P("mod", None, "shard"),
            P("mod", None, "shard"),
            P("mod", None, "shard"),
            P("mod", None, "shard"),
            P("mod", "shard", None),
        ),
        out_specs=(
            P(("mod", "shard"), None),
            P(("mod", "shard"), None),
            P("mod", None, "shard"),
            P("mod", None, "shard"),
            P("mod", "shard", None),
        ),
        check_vma=False,
    )
```

profile of v0, /device:TPU:0, one launch (start us, length us, event | category | flops | bytes accessed | tf_op | source)
XLA Modules:
  0.0 327.6 jit_solution(9912826482816697624)
XLA Ops:
  7.2 0.8 fusion.44
  8.2 0.8 select_reduce_fusion
  9.3 10.2 %all_to_all.25 = bf16[4,6,4096]{2,1,0:T(8,128)(2,1)S(1)} all-to-all(bf16[4,6,4096]{2,1,0:T(8,128)(2,1)S(1)} %reshape.137), channel_id=1, replica_groups=mesh['mod'=4,'shard'=8] {'mod'}, dimensions={0} | all-to-all | bytes 393216 | tf_op jit(solution)/shard_map/all_to_all | solution.py:64
  19.5 0.7 reshape.138
  21.1 8.5 %all_to_all.26 = bf16[4,6,4096]{2,1,0:T(8,128)(2,1)S(1)} all-to-all(bf16[4,6,4096]{2,1,0:T(8,128)(2,1)S(1)} %reshape.134), channel_id=1, replica_groups=mesh['mod'=4,'shard'=8] {'mod'}, dimensions={0} | all-to-all | bytes 393216 | tf_op jit(solution)/shard_map/all_to_all | solution.py:42
  29.6 0.7 reshape.135
  30.7 8.4 %all_to_all.27 = bf16[4,6,4096]{2,1,0:T(8,128)(2,1)S(1)} all-to-all(bf16[4,6,4096]{2,1,0:T(8,128)(2,1)S(1)} %reshape.140), channel_id=1, replica_groups=mesh['mod'=4,'shard'=8] {'mod'}, dimensions={0} | all-to-all | bytes 393216 | tf_op jit(solution)/shard_map/all_to_all | solution.py:63
  39.1 0.8 reshape.141
  39.9 25.0 %all-gather.6.cloned.1.call-done = bf16[192,4096]{1,0:T(8,128)(2,1)} async-done(((bf16[24,4096]{1,0:T(8,128)(2,1)}), bf16[192,4096]{1,0:T(8,128)(2,1)}) %all-gather.6.cloned.1.call-update) | async-done | bytes 1572880 | tf_op jit(solution)/shard_map/all_gather | solution.py:68
  64.9 8.9 %fusion.30 = (bf16[192,1376]{1,0:T(8,128)(2,1)S(1)}, f32[192,1376]{1,0:T(8,128)S(1)}) fusion(bf16[1,192,1376]{2,1,0:T(8,128)(2,1)S(1)} %copy-done.8, bf16[1,192,1376]{2,1,0:T(8,128)(2,1)S(1)} %copy-done.9, bf16[192,4096]{1,0:T(8,128)(2,1)} %all-gather.6.cloned.1.call-done, bf16[1,1376,4096]{2,1,0:T(8,128)(2,1)} %param.19), kind=kOutput, calls=%fused_computation.35 | convolution fusion | flops 2167431168 | bytes 15486976 | tf_op jit(solution)/shard_map/dot_general | solution.py:32
  73.9 6.2 %fusion.7 = f32[192,4096]{1,0:T(8,128)S(1)} fusion(bf16[1,4096,1376]{1,2,0:T(8,128)(2,1)} %param.18, f32[192,1376]{1,0:T(8,128)S(1)} %get-tuple-element.6, bf16[1,192,1376]{2,1,0:T(8,128)(2,1)S(1)} %copy-done.9), kind=kOutput, calls=%fused_computation.10 | convolution fusion | flops 2166110208 | bytes 16003072 | tf_op jit(solution)/shard_map/dot_general | solution.py:32
  80.1 4.5 %fusion.15 = f32[192,4096]{1,0:T(8,128)} fusion(f32[192,4096]{1,0:T(8,128)S(1)} %fusion.7, bf16[192,1376]{1,0:T(8,128)(2,1)S(1)} %get-tuple-element.5, bf16[1,4096,1376]{1,2,0:T(8,128)(2,1)S(1)} %bitcast.80), kind=kOutput, calls=%fused_computation.18 | convolution fusion | flops 2165047296 | bytes 18092032 | tf_op jit(solution)/shard_map/dot_general | solution.py:32
  84.6 0.2 reduce-scatter.3.cloned.1.call-start
  84.9 25.5 %all-gather.4.cloned.1.call-done = bf16[192,4096]{1,0:T(8,128)(2,1)} async-done(((bf16[24,4096]{1,0:T(8,128)(2,1)}), bf16[192,4096]{1,0:T(8,128)(2,1)}) %all-gather.4.cloned.1.call-update) | async-done | bytes 1572880 | tf_op jit(solution)/shard_map/all_gather | solution.py:44
  110.3 9.7 %fusion.13 = f32[192,1376]{1,0:T(8,128)} fusion(bf16[192,4096]{1,0:T(8,128)(2,1)} %all-gather.4.cloned.1.call-done, bf16[1,4096,1376]{1,2,0:T(8,128)(2,1)} %param.17), kind=kOutput, calls=%fused_computation.16 | convolution fusion | flops 2164260864 | bytes 13901824 | tf_op jit(solution)/shard_map/dot_general | solution.py:45
  120.0 15.8 %fusion.5 = f32[192,4096]{1,0:T(8,128)} fusion(bf16[1,1376,4096]{2,1,0:T(8,128)(2,1)} %param.19, bf16[192,4096]{1,0:T(8,128)(2,1)S(1)} %copy-done.7, bf16[1,4096,1376]{1,2,0:T(8,128)(2,1)} %param.18, f32[192,1376]{1,0:T(8,128)} %fusion.13), kind=kOutput, calls=%fused_computation.8 | convolution fusion | flops 4330106880 | bytes 28319744 | tf_op jit(solution)/shard_map/dot_general | solution.py:47
  135.9 1.5 copy-done.6
  137.4 7.1 %fusion = bf16[1,1376,4096]{2,1,0:T(8,128)(2,1)} fusion(bf16[192,4096]{1,0:T(8,128)(2,1)S(1)} %copy-done.6, bf16[1,192,1376]{2,1,0:T(8,128)(2,1)S(1)} %copy-done.8, bf16[1,192,1376]{2,1,0:T(8,128)(2,1)} %param.15), kind=kOutput, calls=%fused_computation.3 | convolution fusion | flops 2172010496 | bytes 13901824 | tf_op jit(solution)/shard_map/dot_general | solution.py:79
  144.6 10.6 %all-gather.8.cloned.1.call-done = bf16[192,4096]{1,0:T(8,128)(2,1)} async-done(((bf16[24,4096]{1,0:T(8,128)(2,1)}), bf16[192,4096]{1,0:T(8,128)(2,1)}) %all-gather.8.cloned.1.call-update) | async-done | bytes 1572880 | tf_op jit(solution)/shard_map/all_gather | solution.py:67
  155.1 9.5 %fusion.2 = bf16[1,4096,1376]{1,2,0:T(8,128)(2,1)} fusion(bf16[192,4096]{1,0:T(8,128)(2,1)} %all-gather.8.cloned.1.call-done, f32[192,1376]{1,0:T(8,128)} %copy-done.10, bf16[1,192,1376]{2,1,0:T(8,128)(2,1)} %param.15), kind=kOutput, calls=%fused_computation.5 | convolution fusion | flops 2171746304 | bytes 14430208 | tf_op jit(solution)/shard_map/dot_general | solution.py:85
  164.6 67.3 %reduce-scatter.5.cloned.1.call-done = f32[24,4096]{1,0:T(8,128)} async-done(((f32[192,4096]{1,0:T(8,128)}), f32[24,4096]{1,0:T(8,128)}) %reduce-scatter.5.cloned.1.call-update) | async-done | bytes 393232 | tf_op jit(solution)/shard_map/reduce_scatter | solution.py:89
  231.9 1.0 convert_element_type.115
  232.9 0.8 reshape.139
  233.7 3.4 %all-to-all-start.3 = ((bf16[4,6,4096]{2,1,0:T(8,128)(2,1)}), bf16[4,6,4096]{2,1,0:T(8,128)(2,1)S(1)}, u32[]{:S(2)}, u32[]{:S(2)}) async-start(bf16[4,6,4096]{2,1,0:T(8,128)(2,1)} %reshape.139), calls=%async_computation.5 | async-start | bytes 524288 | tf_op jit(solution)/shard_map/all_to_all | solution.py:91
  237.1 6.0 %fusion.1 = bf16[1,4096,1376]{1,2,0:T(8,128)(2,1)} fusion(bf16[192,4096]{1,0:T(8,128)(2,1)S(1)} %copy-done.2, bf16[192,1376]{1,0:T(8,128)(2,1)S(1)} %get-tuple-element.5), kind=kOutput, calls=%fused_computation.4 | convolution fusion | flops 2169896960 | bytes 13373440 | tf_op jit(solution)/shard_map/dot_general | solution.py:82
  243.2 65.8 %reduce-scatter.3.cloned.1.call-done = f32[24,4096]{1,0:T(8,128)} async-done(((f32[192,4096]{1,0:T(8,128)}), f32[24,4096]{1,0:T(8,128)}) %reduce-scatter.3.cloned.1.call-update) | async-done | bytes 393232 | tf_op jit(solution)/shard_map/reduce_scatter | solution.py:50
  309.0 1.0 convert_element_type.102
  310.0 0.8 reshape.136
  310.8 3.4 %all-to-all-start.1 = ((bf16[4,6,4096]{2,1,0:T(8,128)(2,1)}), bf16[4,6,4096]{2,1,0:T(8,128)(2,1)S(1)}, u32[]{:S(2)}, u32[]{:S(2)}) async-start(bf16[4,6,4096]{2,1,0:T(8,128)(2,1)} %reshape.136), calls=%async_computation.2 | async-start | bytes 524288 | tf_op jit(solution)/shard_map/all_to_all | solution.py:52
  314.2 0.9 fusion.19
  315.1 5.1 %all-to-all-done.1 = bf16[4,6,4096]{2,1,0:T(8,128)(2,1)S(1)} async-done(((bf16[4,6,4096]{2,1,0:T(8,128)(2,1)}), bf16[4,6,4096]{2,1,0:T(8,128)(2,1)S(1)}, u32[]{:S(2)}, u32[]{:S(2)}) %all-to-all-start.1) | async-done | bytes 196640 | tf_op jit(solution)/shard_map/all_to_all | solution.py:52
  320.2 0.9 fusion.18
  (56 shorter events, 1.6 us)
Async XLA Ops:
  7.2 1.9 copy-start
  7.2 13.1 %copy-start.5 = (s32[16,1]{0,1:T(1,128)S(1)}, s32[16,1]{0,1:T(1,128)}, u32[]{:S(2)}) copy-start(s32[16,1]{0,1:T(1,128)} %param.11) | copy-start | bytes 196
  7.2 13.6 %copy-start.3 = (bf16[16,4096]{1,0:T(8,128)(2,1)S(1)}, bf16[16,4096]{1,0:T(8,128)(2,1)}, u32[]{:S(2)}) copy-start(bf16[16,4096]{1,0:T(8,128)(2,1)} %param.10) | copy-start | bytes 393220
  7.2 57.7 %all-gather.6.cloned.1.call-start = ((), (), s32[]{:S(2)}) async-start(), calls=%async_computation.9 | async-start | bytes 1769472 | tf_op jit(solution)/shard_map/all_gather | solution.py:68
  9.3 21.1 %copy-start.4 = (bf16[16,4096]{1,0:T(8,128)(2,1)S(1)}, bf16[16,4096]{1,0:T(8,128)(2,1)}, u32[]{:S(2)}) copy-start(bf16[16,4096]{1,0:T(8,128)(2,1)} %param.12) | copy-start | bytes 393220
  20.3 90.0 %all-gather.4.cloned.1.call-start = ((), (), s32[]{:S(2)}) async-start(), calls=%async_computation.7 | async-start | bytes 1769472 | tf_op jit(solution)/shard_map/all_gather | solution.py:44
  21.0 43.9 %copy-start.8 = (bf16[1,192,1376]{2,1,0:T(8,128)(2,1)S(1)}, bf16[1,192,1376]{2,1,0:T(8,128)(2,1)}, u32[]{:S(2)}) copy-start(bf16[1,192,1376]{2,1,0:T(8,128)(2,1)} %param.16) | copy-start | bytes 1585156
  21.0 43.9 %copy-start.9 = (bf16[1,192,1376]{2,1,0:T(8,128)(2,1)S(1)}, bf16[1,192,1376]{2,1,0:T(8,128)(2,1)}, u32[]{:S(2)}) copy-start(bf16[1,192,1376]{2,1,0:T(8,128)(2,1)} %param.15) | copy-start | bytes 1585156
  30.4 124.8 %all-gather.8.cloned.1.call-start = ((), (), s32[]{:S(2)}) async-start(), calls=%async_computation.11 | async-start | bytes 1769472 | tf_op jit(solution)/shard_map/all_gather | solution.py:67
  39.9 192.0 %reduce-scatter.5.cloned.1.call-start = ((), (), s32[]{:S(2)}) async-start(), calls=%async_computation.10 | async-start | bytes 3538944 | tf_op jit(solution)/shard_map/reduce_scatter | solution.py:89
  64.9 15.2 %slice-start = ((s8[11272192]{0:T(1024)(128)(4,1)}), s8[4194304]{0:T(1024)(128)(4,1)S(1)}, s32[]{:S(2)}) async-start(s8[11272192]{0:T(1024)(128)(4,1)} %bitcast.79), calls=%async_computation.12 | async-start | bytes 8388608
  64.9 15.2 %slice-start.1 = ((s8[11272192]{0:T(1024)(128)(4,1)}), s8[2883584]{0:T(1024)(128)(4,1)S(1)}, s32[]{:S(2)}) async-start(s8[11272192]{0:T(1024)(128)(4,1)} %bitcast.79), calls=%async_computation.13 | async-start | bytes 5767168
  73.8 6.3 %copy-start.10 = (f32[192,1376]{1,0:T(8,128)}, f32[192,1376]{1,0:T(8,128)S(1)}, u32[]{:S(2)}) copy-start(f32[192,1376]{1,0:T(8,128)S(1)} %get-tuple-element.6) | copy-start | bytes 3170308
  73.9 6.3 %slice-start.2 = ((s8[11272192]{0:T(1024)(128)(4,1)}), s8[4194304]{0:T(1024)(128)(4,1)S(1)}, s32[]{:S(2)}) async-start(s8[11272192]{0:T(1024)(128)(4,1)} %bitcast.79), calls=%async_computation.14 | async-start | bytes 8388608
  84.6 224.4 %reduce-scatter.3.cloned.1.call-start = ((), (), s32[]{:S(2)}) async-start(), calls=%async_computation.8 | async-start | bytes 3538944 | tf_op jit(solution)/shard_map/reduce_scatter | solution.py:50
  110.3 9.7 %copy-start.7 = (bf16[192,4096]{1,0:T(8,128)(2,1)S(1)}, bf16[192,4096]{1,0:T(8,128)(2,1)}, u32[]{:S(2)}) copy-start(bf16[192,4096]{1,0:T(8,128)(2,1)} %all-gather.4.cloned.1.call-done) | copy-start | bytes 4718596
  135.9 1.6 copy-start.6
  155.1 82.0 %copy-start.2 = (bf16[192,4096]{1,0:T(8,128)(2,1)S(1)}, bf16[192,4096]{1,0:T(8,128)(2,1)}, u32[]{:S(2)}) copy-start(bf16[192,4096]{1,0:T(8,128)(2,1)} %all-gather.8.cloned.1.call-done) | copy-start | bytes 4718596
  233.7 77.1 %all-to-all-start.3 = ((bf16[4,6,4096]{2,1,0:T(8,128)(2,1)}), bf16[4,6,4096]{2,1,0:T(8,128)(2,1)S(1)}, u32[]{:S(2)}, u32[]{:S(2)}) async-start(bf16[4,6,4096]{2,1,0:T(8,128)(2,1)} %reshape.139), calls=%async_computation.5 | async-start | bytes 524288 | tf_op jit(solution)/shard_map/all_to_all | solution.py:91
  237.1 83.9 %copy-start.1 = (bf16[16,4096]{1,0:T(8,128)(2,1)S(1)}, bf16[16,4096]{1,0:T(8,128)(2,1)}, u32[]{:S(2)}) copy-start(bf16[16,4096]{1,0:T(8,128)(2,1)} %param.14) | copy-start | bytes 393220
  310.8 9.4 %all-to-all-start.1 = ((bf16[4,6,4096]{2,1,0:T(8,128)(2,1)}), bf16[4,6,4096]{2,1,0:T(8,128)(2,1)S(1)}, u32[]{:S(2)}, u32[]{:S(2)}) async-start(bf16[4,6,4096]{2,1,0:T(8,128)(2,1)} %reshape.136), calls=%async_computation.2 | async-start | bytes 524288 | tf_op jit(solution)/shard_map/all_to_all | solution.py:52
Sparse Core Ops, SparseCore 0:
  20.4 44.4 all-gather.5
  67.7 42.5 all-gather.3
  112.5 42.5 all-gather.7
  159.1 72.7 reduce-scatter.4
  235.3 73.6 reduce-scatter.2
where the time goes:
time: 328 us
  waiting for transfers between devices  199 us (61%)
  matrix products  70.1 us (21%)
  blocking collectives  27.1 us (8%)
  between operations  14 us (4%)
  starting transfers between devices  7.2 us (2%)
  local copies, waits for them, and re-layouts  5.84 us (2%)
  other arithmetic  4.02 us (1%)
    reduce_scatter x1, waiting for transfers between devices, backward_pass(): summed = lax.psum_scatter(terms, 'shard', scatter_dimension=0, tiled=True)  67.3 us
    reduce_scatter x1, waiting for transfers between devices, forward_pass(): summed = lax.psum_scatter(terms, 'shard', scatter_dimension=0, tiled=True)  65.8 us
    all_gather x1, waiting for transfers between devices, forward_pass(): piece = lax.all_gather(local_rows, 'shard', axis=0, tiled=True)  25.5 us
    all_gather x1, waiting for transfers between devices, backward_pass(): lax.all_gather(arrived_g.reshape(modes * CAP, width), 'shard', axis=0, ti...  25 us
    dot_general x3, matrix products, contract_last(): lax.dot_general(left, right, (((1,), (1,)), ((), ())), preferred_element_...  19.6 us
    dot_general x1, matrix products, forward_pass(): jnp.dot((jax.nn.silu(gate) * up).astype(jnp.bfloat16), down_w, preferred_...  15.8 us
    all_gather x1, waiting for transfers between devices, backward_pass(): lax.all_gather(arrived_x.reshape(modes * CAP, width), 'shard', axis=0, ti...  10.6 us
    all_to_all x1, blocking collectives, backward_pass(): lax.all_to_all(sent_g, 'mod', split_axis=0, concat_axis=0, tiled=True)  10.2 us
  transfers between devices with their start and end apart: 7, of which 6 were waited for; matrix products, arithmetic and copies ran while one was open for 23% of the time, Pallas kernels for 0%

commit v1 on v0

--- a/solution.py
+++ b/solution.py
@@ -41,7 +41,18 @@
     sent = dispatch(place, tokens_b, modes)
     arrived = lax.all_to_all(sent, "mod", split_axis=0, concat_axis=0, tiled=True)
     local_rows = arrived.reshape(modes * CAP, width)
-    piece = lax.all_gather(local_rows, "shard", axis=0, tiled=True)
+    current_arr = lax.axis_size("shard")
+    small = lax.axis_index("shard")
+    last, step_out, b_next = (current_arr, small, local_rows.shape[0])
+    x_now, x_next = (local_rows, 1)
+    while x_next < last:
+        lanes = []
+        for k in range(last):
+            lanes.append((k, (k - x_next) % last))
+        z_new = lax.ppermute(x_now, "shard", lanes)
+        x_now = jnp.concatenate([x_now, z_new], axis=0)
+        x_next = 2 * x_next
+    piece = jnp.roll(x_now, shift=step_out * b_next, axis=0)
     gate = jnp.dot(piece, gate_w, preferred_element_type=jnp.float32)
     up = jnp.dot(piece, up_w, preferred_element_type=jnp.float32)
     terms = jnp.dot(

time: 328 us -> 308 us (0.939)
  waiting for transfers between devices: 199 us -> 177 us
  blocking collectives: 27.1 us -> 18.6 us
  starting transfers between devices: 7.2 us -> 15.7 us
    ppermute x0 -> x3, waiting for transfers between devices: none -> 55.5 us  [forward_pass(): z_new = lax.ppermute(x_now, 'shard', lanes)]
    all_gather x1 -> x0, waiting for transfers between devices: 25.5 us -> none  [forward_pass(): piece = lax.all_gather(local_rows, 'shard', axis=0, tiled=True)]
    all_gather x1, waiting for transfers between devices: 25 us -> 0.02 us  [backward_pass(): lax.all_gather(arrived_g.reshape(modes * CAP, width), 'shard', axis=0, ti...]
    reduce_scatter x1, waiting for transfers between devices: 65.8 us -> 44.7 us  [forward_pass(): summed = lax.psum_scatter(terms, 'shard', scatter_dimension=0, tiled=True)]
    all_gather x1, waiting for transfers between devices: 10.6 us -> 0.01 us  [backward_pass(): lax.all_gather(arrived_x.reshape(modes * CAP, width), 'shard', axis=0, ti...]
    all_to_all x1 -> x0, blocking collectives: 8.39 us -> none  [backward_pass(): lax.all_to_all(sent_x, 'mod', split_axis=0, concat_axis=0, tiled=True)]
    all_to_all x0 -> x1, waiting for transfers between devices: none -> 5.9 us  [backward_pass(): lax.all_to_all(sent_x, 'mod', split_axis=0, concat_axis=0, tiled=True)]
    ppermute x0 -> x3, starting transfers between devices: none -> 5.18 us  [forward_pass(): z_new = lax.ppermute(x_now, 'shard', lanes)]
  transfers between devices with their start and end apart: 7 -> 10, of which waited for: 6 -> 6; matrix products, arithmetic and copies ran while one was open for 23% -> 24% of each run, Pallas kernels for 0% -> 0%
where the time goes in v1:
time: 308 us; the launch traced here: 307 us
  waiting for transfers between devices  177 us (57%)
  matrix products  68.9 us (22%)
  blocking collectives  18.6 us (6%)
  starting transfers between devices  15.7 us (5%)
  between operations  14.1 us (5%)
  local copies, waits for them, and re-layouts  8.52 us (3%)
  other arithmetic  4.1 us (1%)
    reduce_scatter x1, waiting for transfers between devices, backward_pass(): summed = lax.psum_scatter(terms, 'shard', scatter_dimension=0, tiled=True)  65.7 us
    ppermute x3, waiting for transfers between devices, forward_pass(): z_new = lax.ppermute(x_now, 'shard', lanes)  55.5 us
    reduce_scatter x1, waiting for transfers between devices, forward_pass(): summed = lax.psum_scatter(terms, 'shard', scatter_dimension=0, tiled=True)  44.7 us
    dot_general x3, matrix products, contract_last(): lax.dot_general(left, right, (((1,), (1,)), ((), ())), preferred_element_...  19.5 us
    dot_general x1, matrix products, forward_pass(): jnp.dot((jax.nn.silu(gate) * up).astype(jnp.bfloat16), down_w, preferred_...  16.1 us
    all_to_all x1, blocking collectives, backward_pass(): lax.all_to_all(sent_g, 'mod', split_axis=0, concat_axis=0, tiled=True)  10.2 us
    dot_general x1, matrix products, backward_pass(): lax.dot_general(all_x, dup, outer, preferred_element_type=jnp.float32)  9.5 us
    all_to_all x1, blocking collectives, forward_pass(): lax.all_to_all(sent, 'mod', split_axis=0, concat_axis=0, tiled=True)  8.39 us
  transfers between devices with their start and end apart: 10, of which 6 were waited for; matrix products, arithmetic and copies ran while one was open for 24% of the time, Pallas kernels for 0%

profile of v1, /device:TPU:0, one launch (start us, length us, event | category | flops | bytes accessed | tf_op | source)
XLA Modules:
  0.0 306.8 jit_solution(11145825640326335400)
XLA Ops:
  7.2 0.8 fusion.41
  8.2 0.8 select_reduce_fusion
  9.3 10.2 %all_to_all.25 = bf16[4,6,4096]{2,1,0:T(8,128)(2,1)S(1)} all-to-all(bf16[4,6,4096]{2,1,0:T(8,128)(2,1)S(1)} %reshape.137), channel_id=1, replica_groups=mesh['mod'=4,'shard'=8] {'mod'}, dimensions={0} | all-to-all | bytes 393216 | tf_op jit(solution)/shard_map/all_to_all | solution.py:75
  21.0 8.4 %all_to_all.26 = bf16[4,6,4096]{2,1,0:T(8,128)(2,1)S(1)} all-to-all(bf16[4,6,4096]{2,1,0:T(8,128)(2,1)S(1)} %reshape.134), channel_id=1, replica_groups=mesh['mod'=4,'shard'=8] {'mod'}, dimensions={0} | all-to-all | bytes 393216 | tf_op jit(solution)/shard_map/all_to_all | solution.py:42
  29.4 4.6 %collective-permute-start = (bf16[24,4096]{1,0:T(8,128)(2,1)S(1)}, bf16[24,4096]{1,0:T(8,128)(2,1)S(1)}, u32[]{:S(2)}, u32[]{:S(2)}) collective-permute-start(bf16[24,4096]{1,0:T(8,128)(2,1)S(1)} %reshape.135), channel_id=1, source_target_pairs={{0,7},{1,0},{2,1},{3,2},{4,3},{5,4},{6,5},{7,6},{8,15},{9,8},{10,9... | collective-permute-start | bytes 589832 | tf_op jit(solution)/shard_map/ppermute | solution.py:52
  34.3 0.8 reshape.140
  35.0 3.4 %all-to-all-start.4 = ((bf16[4,6,4096]{2,1,0:T(8,128)(2,1)}), bf16[4,6,4096]{2,1,0:T(8,128)(2,1)S(1)}, u32[]{:S(2)}, u32[]{:S(2)}) async-start(bf16[4,6,4096]{2,1,0:T(8,128)(2,1)} %reshape.140), calls=%async_computation.6 | async-start | bytes 524288 | tf_op jit(solution)/shard_map/all_to_all | solution.py:74
  38.5 5.9 %all-to-all-done.4 = bf16[4,6,4096]{2,1,0:T(8,128)(2,1)S(1)} async-done(((bf16[4,6,4096]{2,1,0:T(8,128)(2,1)}), bf16[4,6,4096]{2,1,0:T(8,128)(2,1)S(1)}, u32[]{:S(2)}, u32[]{:S(2)}) %all-to-all-start.4) | async-done | bytes 196640 | tf_op jit(solution)/shard_map/all_to_all | solution.py:74
  45.8 22.7 %collective-permute-done.1 = bf16[48,4096]{1,0:T(8,128)(2,1)S(1)} collective-permute-done((bf16[48,4096]{1,0:T(8,128)(2,1)S(1)}, bf16[48,4096]{1,0:T(8,128)(2,1)S(1)}, u32[]{:S(2)}, u32[]{:S(2)}) %collective-permute-start.1) | collective-permute-done | bytes 393248 | tf_op jit(solution)/shard_map/ppermute | solution.py:52
  68.7 32.7 %collective-permute-done.2 = bf16[96,4096]{1,0:T(8,128)(2,1)S(1)} collective-permute-done((bf16[96,4096]{1,0:T(8,128)(2,1)S(1)}, bf16[96,4096]{1,0:T(8,128)(2,1)S(1)}, u32[]{:S(2)}, u32[]{:S(2)}) %collective-permute-start.2) | collective-permute-done | bytes 786464 | tf_op jit(solution)/shard_map/ppermute | solution.py:52
  101.7 1.7 copy-done.5
  103.3 8.2 %fusion.9 = f32[192,1376]{1,0:T(8,128)S(1)} fusion(bf16[1,4096,1376]{1,2,0:T(8,128)(2,1)} %param.18, bf16[384,4096]{1,0:T(8,128)(2,1)S(1)} %constant_dynamic-update-slice_fusion, s32[]{:T(128)S(6)} %select_n.14), kind=kOutput, calls=%fused_computation.12 | convolution fusion | flops 2164260864 | bytes 13901828 | tf_op jit(solution)/shard_map/dot_general | solution.py:57
  111.6 16.1 %fusion.5 = f32[192,4096]{1,0:T(8,128)} fusion(bf16[1,1376,4096]{2,1,0:T(8,128)(2,1)} %param.19, f32[192,1376]{1,0:T(8,128)S(1)} %fusion.9, bf16[1,4096,1376]{1,2,0:T(8,128)(2,1)} %param.17, bf16[384,4096]{1,0:T(8,128)(2,1)} %copy-done.5, s32[]{:T(128)S(6)} %select_n.14), kind=kOutput, calls=%fused_computation.8 | convolution fusion | flops 4330106880 | bytes 28319748 | tf_op jit(solution)/shard_map/dot_general | solution.py:58
  128.0 0.8 copy-done.8
  128.9 8.9 %fusion.24 = (bf16[192,1376]{1,0:T(8,128)(2,1)S(1)}, f32[192,1376]{1,0:T(8,128)S(1)}) fusion(bf16[1,192,1376]{2,1,0:T(8,128)(2,1)S(1)} %copy-done.8, bf16[1,192,1376]{2,1,0:T(8,128)(2,1)S(1)} %copy-done.9, bf16[192,4096]{1,0:T(8,128)(2,1)} %all-gather.3.cloned.1.call-done, bf16[1,1376,4096]{2,1,0:T(8,128)(2,1)} %param.19), kind=kOutput, calls=%fused_computation.35 | convolution fusion | flops 2167431168 | bytes 15486976 | tf_op jit(solution)/shard_map/dot_general | solution.py:32
  137.9 6.2 %fusion.7 = f32[192,4096]{1,0:T(8,128)S(1)} fusion(bf16[1,4096,1376]{1,2,0:T(8,128)(2,1)} %param.18, f32[192,1376]{1,0:T(8,128)S(1)} %get-tuple-element.6, bf16[1,192,1376]{2,1,0:T(8,128)(2,1)S(1)} %copy-done.9), kind=kOutput, calls=%fused_computation.10 | convolution fusion | flops 2166110208 | bytes 16003072 | tf_op jit(solution)/shard_map/dot_general | solution.py:32
  144.1 4.4 %fusion.15 = f32[192,4096]{1,0:T(8,128)} fusion(f32[192,4096]{1,0:T(8,128)S(1)} %fusion.7, bf16[192,1376]{1,0:T(8,128)(2,1)S(1)} %get-tuple-element.5, bf16[1,4096,1376]{1,2,0:T(8,128)(2,1)S(1)} %bitcast.76), kind=kOutput, calls=%fused_computation.18 | convolution fusion | flops 2165047296 | bytes 18092032 | tf_op jit(solution)/shard_map/dot_general | solution.py:32
  148.6 1.4 copy-done.7
  149.9 7.1 %fusion = bf16[1,1376,4096]{2,1,0:T(8,128)(2,1)} fusion(bf16[192,4096]{1,0:T(8,128)(2,1)S(1)} %copy-done.7, bf16[1,192,1376]{2,1,0:T(8,128)(2,1)S(1)} %copy-done.8, bf16[1,192,1376]{2,1,0:T(8,128)(2,1)} %param.15), kind=kOutput, calls=%fused_computation.3 | convolution fusion | flops 2172010496 | bytes 13901824 | tf_op jit(solution)/shard_map/dot_general | solution.py:90
  157.1 9.5 %fusion.2 = bf16[1,4096,1376]{1,2,0:T(8,128)(2,1)} fusion(bf16[192,4096]{1,0:T(8,128)(2,1)} %all-gather.5.cloned.1.call-done, f32[192,1376]{1,0:T(8,128)} %copy-done.10, bf16[1,192,1376]{2,1,0:T(8,128)(2,1)} %param.15), kind=kOutput, calls=%fused_computation.5 | convolution fusion | flops 2171746304 | bytes 14430208 | tf_op jit(solution)/shard_map/dot_general | solution.py:96
  166.6 44.7 %reduce-scatter.3.cloned.1.call-done = f32[24,4096]{1,0:T(8,128)} async-done(((f32[192,4096]{1,0:T(8,128)}), f32[24,4096]{1,0:T(8,128)}) %reduce-scatter.3.cloned.1.call-update) | async-done | bytes 393232 | tf_op jit(solution)/shard_map/reduce_scatter | solution.py:61
  211.3 1.0 convert_element_type.102
  212.3 0.8 reshape.136
  213.1 3.4 %all-to-all-start.1 = ((bf16[4,6,4096]{2,1,0:T(8,128)(2,1)}), bf16[4,6,4096]{2,1,0:T(8,128)(2,1)S(1)}, u32[]{:S(2)}, u32[]{:S(2)}) async-start(bf16[4,6,4096]{2,1,0:T(8,128)(2,1)} %reshape.136), calls=%async_computation.2 | async-start | bytes 524288 | tf_op jit(solution)/shard_map/all_to_all | solution.py:63
  216.5 6.0 %fusion.1 = bf16[1,4096,1376]{1,2,0:T(8,128)(2,1)} fusion(bf16[192,4096]{1,0:T(8,128)(2,1)S(1)} %copy-done.2, bf16[192,1376]{1,0:T(8,128)(2,1)S(1)} %get-tuple-element.5), kind=kOutput, calls=%fused_computation.4 | convolution fusion | flops 2169896960 | bytes 13373440 | tf_op jit(solution)/shard_map/dot_general | solution.py:93
  222.5 65.7 %reduce-scatter.5.cloned.1.call-done = f32[24,4096]{1,0:T(8,128)} async-done(((f32[192,4096]{1,0:T(8,128)}), f32[24,4096]{1,0:T(8,128)}) %reduce-scatter.5.cloned.1.call-update) | async-done | bytes 393232 | tf_op jit(solution)/shard_map/reduce_scatter | solution.py:100
  288.2 1.0 convert_element_type.115
  289.3 0.8 reshape.139
  290.0 3.4 %all-to-all-start.3 = ((bf16[4,6,4096]{2,1,0:T(8,128)(2,1)}), bf16[4,6,4096]{2,1,0:T(8,128)(2,1)S(1)}, u32[]{:S(2)}, u32[]{:S(2)}) async-start(bf16[4,6,4096]{2,1,0:T(8,128)(2,1)} %reshape.139), calls=%async_computation.5 | async-start | bytes 524288 | tf_op jit(solution)/shard_map/all_to_all | solution.py:102
  293.4 0.9 fusion.18
  294.3 5.1 %all-to-all-done.3 = bf16[4,6,4096]{2,1,0:T(8,128)(2,1)S(1)} async-done(((bf16[4,6,4096]{2,1,0:T(8,128)(2,1)}), bf16[4,6,4096]{2,1,0:T(8,128)(2,1)S(1)}, u32[]{:S(2)}, u32[]{:S(2)}) %all-to-all-start.3) | async-done | bytes 196640 | tf_op jit(solution)/shard_map/all_to_all | solution.py:102
  299.4 0.9 fusion.19
  (70 shorter events, 4.4 us)
Async XLA Ops:
  7.2 1.9 copy-start
  7.2 13.1 %copy-start.6 = (s32[16,1]{0,1:T(1,128)S(1)}, s32[16,1]{0,1:T(1,128)}, u32[]{:S(2)}) copy-start(s32[16,1]{0,1:T(1,128)} %param.11) | copy-start | bytes 196
  7.2 13.5 %copy-start.3 = (bf16[16,4096]{1,0:T(8,128)(2,1)S(1)}, bf16[16,4096]{1,0:T(8,128)(2,1)}, u32[]{:S(2)}) copy-start(bf16[16,4096]{1,0:T(8,128)(2,1)} %param.10) | copy-start | bytes 393220
  7.2 120.8 %all-gather.3.cloned.1.call-start = ((), (), s32[]{:S(2)}) async-start(), calls=%async_computation.8 | async-start | bytes 1769472 | tf_op jit(solution)/shard_map/all_gather | solution.py:79
  9.3 24.7 %copy-start.4 = (bf16[16,4096]{1,0:T(8,128)(2,1)S(1)}, bf16[16,4096]{1,0:T(8,128)(2,1)}, u32[]{:S(2)}) copy-start(bf16[16,4096]{1,0:T(8,128)(2,1)} %param.12) | copy-start | bytes 393220
  29.4 15.8 %collective-permute-start = (bf16[24,4096]{1,0:T(8,128)(2,1)S(1)}, bf16[24,4096]{1,0:T(8,128)(2,1)S(1)}, u32[]{:S(2)}, u32[]{:S(2)}) collective-permute-start(bf16[24,4096]{1,0:T(8,128)(2,1)S(1)} %reshape.135), channel_id=1, source_target_pairs={{0,7},{1,0},{2,1},{3,2},{4,3},{5,4},{6,5},{7,6},{8,15},{9,8},{10,9... | collective-permute-start | bytes 589832 | tf_op jit(solution)/shard_map/ppermute | solution.py:52
  35.0 9.4 %all-to-all-start.4 = ((bf16[4,6,4096]{2,1,0:T(8,128)(2,1)}), bf16[4,6,4096]{2,1,0:T(8,128)(2,1)S(1)}, u32[]{:S(2)}, u32[]{:S(2)}) async-start(bf16[4,6,4096]{2,1,0:T(8,128)(2,1)} %reshape.140), calls=%async_computation.6 | async-start | bytes 524288 | tf_op jit(solution)/shard_map/all_to_all | solution.py:74
  38.4 118.6 %all-gather.5.cloned.1.call-start = ((), (), s32[]{:S(2)}) async-start(), calls=%async_computation.10 | async-start | bytes 1769472 | tf_op jit(solution)/shard_map/all_gather | solution.py:78
  45.2 166.1 %reduce-scatter.3.cloned.1.call-start = ((), (), s32[]{:S(2)}) async-start(), calls=%async_computation.7 | async-start | bytes 3538944 | tf_op jit(solution)/shard_map/reduce_scatter | solution.py:61
  45.3 23.2 %collective-permute-start.1 = (bf16[48,4096]{1,0:T(8,128)(2,1)S(1)}, bf16[48,4096]{1,0:T(8,128)(2,1)S(1)}, u32[]{:S(2)}, u32[]{:S(2)}) collective-permute-start(bf16[48,4096]{1,0:T(8,128)(2,1)S(1)} %pad_maximum_fusion.1), channel_id=1, source_target_pairs={{0,6},{1,7},{2,0},{3,1},{4,2},{5,3},{6,4},{7,5},{8,14},{9,15},{10,... | collective-permute-start | bytes 1179656 | tf_op jit(solution)/shard_map/ppermute | solution.py:52
  68.6 32.9 %collective-permute-start.2 = (bf16[96,4096]{1,0:T(8,128)(2,1)S(1)}, bf16[96,4096]{1,0:T(8,128)(2,1)S(1)}, u32[]{:S(2)}, u32[]{:S(2)}) collective-permute-start(bf16[96,4096]{1,0:T(8,128)(2,1)S(1)} %pad_maximum_fusion), channel_id=1, source_target_pairs={{0,4},{1,5},{2,6},{3,7},{4,0},{5,1},{6,2},{7,3},{8,12},{9,13},{10,... | collective-permute-start | bytes 2359304 | tf_op jit(solution)/shard_map/ppermute | solution.py:52
  101.7 1.7 copy-start.5
  127.7 1.1 copy-start.8
  127.7 1.2 copy-start.9
  127.7 160.5 %reduce-scatter.5.cloned.1.call-start = ((), (), s32[]{:S(2)}) async-start(), calls=%async_computation.9 | async-start | bytes 3538944 | tf_op jit(solution)/shard_map/reduce_scatter | solution.py:100
  128.9 15.1 %slice-start = ((s8[11272192]{0:T(1024)(128)(4,1)}), s8[4194304]{0:T(1024)(128)(4,1)S(1)}, s32[]{:S(2)}) async-start(s8[11272192]{0:T(1024)(128)(4,1)} %bitcast.75), calls=%async_computation.11 | async-start | bytes 8388608
  128.9 15.1 %slice-start.1 = ((s8[11272192]{0:T(1024)(128)(4,1)}), s8[2883584]{0:T(1024)(128)(4,1)S(1)}, s32[]{:S(2)}) async-start(s8[11272192]{0:T(1024)(128)(4,1)} %bitcast.75), calls=%async_computation.12 | async-start | bytes 5767168
  137.8 6.2 %copy-start.10 = (f32[192,1376]{1,0:T(8,128)}, f32[192,1376]{1,0:T(8,128)S(1)}, u32[]{:S(2)}) copy-start(f32[192,1376]{1,0:T(8,128)S(1)} %get-tuple-element.6) | copy-start | bytes 3170308
  137.8 6.2 %slice-start.2 = ((s8[11272192]{0:T(1024)(128)(4,1)}), s8[4194304]{0:T(1024)(128)(4,1)S(1)}, s32[]{:S(2)}) async-start(s8[11272192]{0:T(1024)(128)(4,1)} %bitcast.75), calls=%async_computation.13 | async-start | bytes 8388608
  148.5 1.4 copy-start.7
  157.1 59.4 %copy-start.2 = (bf16[192,4096]{1,0:T(8,128)(2,1)S(1)}, bf16[192,4096]{1,0:T(8,128)(2,1)}, u32[]{:S(2)}) copy-start(bf16[192,4096]{1,0:T(8,128)(2,1)} %all-gather.5.cloned.1.call-done) | copy-start | bytes 4718596
  213.1 77.0 %all-to-all-start.1 = ((bf16[4,6,4096]{2,1,0:T(8,128)(2,1)}), bf16[4,6,4096]{2,1,0:T(8,128)(2,1)S(1)}, u32[]{:S(2)}, u32[]{:S(2)}) async-start(bf16[4,6,4096]{2,1,0:T(8,128)(2,1)} %reshape.136), calls=%async_computation.2 | async-start | bytes 524288 | tf_op jit(solution)/shard_map/all_to_all | solution.py:63
  216.5 83.8 %copy-start.1 = (bf16[16,4096]{1,0:T(8,128)(2,1)S(1)}, bf16[16,4096]{1,0:T(8,128)(2,1)}, u32[]{:S(2)}) copy-start(bf16[16,4096]{1,0:T(8,128)(2,1)} %param.14) | copy-start | bytes 393220
  290.0 9.4 %all-to-all-start.3 = ((bf16[4,6,4096]{2,1,0:T(8,128)(2,1)}), bf16[4,6,4096]{2,1,0:T(8,128)(2,1)S(1)}, u32[]{:S(2)}, u32[]{:S(2)}) async-start(bf16[4,6,4096]{2,1,0:T(8,128)(2,1)} %reshape.139), calls=%async_computation.5 | async-start | bytes 524288 | tf_op jit(solution)/shard_map/all_to_all | solution.py:102
Sparse Core Ops, SparseCore 0:
  20.4 50.1 all-gather.2
  72.7 61.6 all-gather.4
  138.6 72.6 reduce-scatter.2
  214.7 73.4 reduce-scatter.4
